TPU v7x, 128 devices: a whole 4x4x4 slice. The times are simulated.
128 devices in a mesh: freq: 8 (over x, z_hi), space: 16 (over z_lo, y, core).
Axes of the slice: x: 4, y: 4, z: 4 (z_hi: 2, z_lo: 2; z = z_hi * 2 + z_lo), core: 2. Of those that a mesh axis runs over, the one named last changes fastest.
Arguments:
- spectra: bfloat16 [128, 49152, 256], P('freq', 'space'), may hold values from -48 to 48, as said below
- weight: float32 [49152], P('space'), may hold values from 0.25 to 4
- partner: int32 [128], P('freq'), may hold values from 0 to 15
- counts: int32 [128], P('freq'), may hold values from 1 to 8
Outputs:
- modes: bfloat16 [128, 16, 49152], P('freq', None, 'space')
- energy: float32 [128, 8], P('freq')
- coherence: float32 [128, 2, 8, 8], P('freq')
Inputs may be any that keep to these rules, and one draw needn't show every extreme that they name: spectra are finite Fourier coefficients.
All inputs are finite; a program needn't handle non-finite values.
Results may differ from a plain program's by a relative error of at most 0.0045.
Values may be sent and summed in bfloat16 or wider, within the bound.
A program may use at most 128 MiB of HBM per device.

v0:
```python
import jax
import jax.numpy as jnp
from jax import lax
from jax.sharding import PartitionSpec as P

KMAX = 8
ITERS = 4


def cut_along(array, dim, size):
    shape = array.shape
    parts = array.reshape(*shape[:dim], size, shape[dim] // size, *shape[dim + 1 :])
    return jnp.moveaxis(parts, dim, 0)


def edges_of(length, count):
    unit = 8 if length >= 8 * count else 1
    return [length // unit * k // count * unit for k in range(1, count)]


def laid_out(parts, dim):
    shape = list(parts.shape[1:])
    shape[dim] *= parts.shape[0]
    return jnp.moveaxis(parts, 0, dim).reshape(shape)


def cut_exchange(array, axis, pieces, split_dim, concat_dim):
    parts = cut_along(array, split_dim, lax.axis_size(axis))
    split_at = max(range(1, max(2, parts.ndim - 1)), key=lambda d: parts.shape[d])
    outs = []
    for share in jnp.split(parts, edges_of(parts.shape[split_at], pieces), axis=split_at):
        if share.size:
            outs.append(lax.all_to_all(share, axis, split_axis=0, concat_axis=0, tiled=True))
    return laid_out(jnp.concatenate(outs, axis=split_at), concat_dim)


def copy_for_each(array, axis):
    size = lax.axis_size(axis)
    return lax.all_to_all(
        jnp.broadcast_to(array[None], (size, *array.shape)), axis, 0, 0, tiled=True
    )


def gathered_copies(array, axis, dim):
    return laid_out(copy_for_each(array, axis), dim)


def summed_on_arrival(array, axis, dim):
    size = lax.axis_size(axis)
    parts = lax.all_to_all(cut_along(array, dim, size), axis, 0, 0, tiled=True)
    return jnp.sum(parts.astype(jnp.float32), axis=0)


def taken_together(array, axis):
    return copy_for_each(array, axis).sum(axis=0)


def embed(gram_re, gram_im):
    top = jnp.concatenate([gram_re, -gram_im], axis=2)
    bottom = jnp.concatenate([gram_im, gram_re], axis=2)
    return jnp.concatenate([top, bottom], axis=1)


def apply_operator(operator, basis):
    return jnp.einsum("fkc,fdc->fkd", basis, operator, precision=lax.Precision.HIGHEST)


def orthonormal(vectors, half):
    done = []
    for index in range(vectors.shape[1]):
        vector = vectors[:, index, :]
        for earlier in done:
            early_re, early_im = (earlier[:, :half], earlier[:, half:])
            vec_re, vec_im = (vector[:, :half], vector[:, half:])
            proj_re = jnp.sum(early_re * vec_re + early_im * vec_im, axis=1, keepdims=True)
            proj_im = jnp.sum(early_re * vec_im - early_im * vec_re, axis=1, keepdims=True)
            new_re = vec_re - proj_re * early_re + proj_im * early_im
            new_im = vec_im - proj_re * early_im - proj_im * early_re
            vector = jnp.concatenate([new_re, new_im], axis=1)
        length = jnp.sqrt(jnp.sum(vector * vector, axis=1, keepdims=True) + 1e-06)
        done.append(vector / length)
    return jnp.stack(done, axis=1)


def solve(gram_re, gram_im):
    half = gram_re.shape[1]
    operator = embed(gram_re, gram_im)
    basis = jnp.broadcast_to(
        jnp.eye(KMAX, 2 * half, dtype=jnp.float32), (gram_re.shape[0], KMAX, 2 * half)
    )
    for sweep in range(ITERS):
        basis = orthonormal(apply_operator(operator, basis), half)
    image = apply_operator(operator, basis)
    energy = jnp.sum(basis * image, axis=2)
    return (basis, energy)


def combine(moments, half, total):
    gram_re = (moments[:, :half, :half] + moments[:, half:, half:]) / total
    gram_im = (moments[:, :half, half:] - moments[:, half:, :half]) / total
    return (gram_re, gram_im)


def coefficients(basis, energy, counts):
    half = basis.shape[2] // 2
    ranks = jnp.arange(KMAX, dtype=jnp.int32)[None, :]
    scale = jnp.where(ranks < counts[:, None], 1.0 / jnp.sqrt(energy + 1e-06), 0.0)[:, :, None]
    part_re, part_im = (basis[:, :, :half], basis[:, :, half:])
    upper = jnp.concatenate([part_re, -part_im], axis=2) * scale
    lower = jnp.concatenate([part_im, part_re], axis=2) * scale
    return jnp.concatenate([upper, lower], axis=1).astype(jnp.bfloat16)


def cross_terms(own_modes, other_modes, point_weight, total):
    phi = own_modes.astype(jnp.float32)
    psi = other_modes.astype(jnp.float32)
    wphi = phi * point_weight[None, None, :]
    highest = lax.Precision.HIGHEST

    def inner(left, right):
        return jnp.einsum("fkp,flp->fkl", left, right, precision=highest)

    real_part = inner(wphi[:, :KMAX], psi[:, :KMAX]) + inner(wphi[:, KMAX:], psi[:, KMAX:])
    imag_part = inner(wphi[:, :KMAX], psi[:, KMAX:]) - inner(wphi[:, KMAX:], psi[:, :KMAX])
    return jnp.stack([real_part, imag_part], axis=1) / total


def on_device(spectra, weight, partner, counts):
    groups = spectra.shape[0]
    half = spectra.shape[2] // 2
    total = spectra.shape[1] * lax.axis_size("space")
    weighted = (weight[None, :, None] * spectra).astype(jnp.bfloat16)
    moments = lax.dot_general(
        spectra, weighted, (((1,), (1,)), ((0,), (0,))), preferred_element_type=jnp.float32
    )
    local_re, local_im = combine(moments, half, total)
    gram_re, gram_im = lax.psum((local_re, local_im), "space")
    basis, energy = solve(gram_re, gram_im)
    coefficient = coefficients(basis, energy, counts)
    modes = jnp.einsum(
        "fkc,fpc->fkp", coefficient, spectra, preferred_element_type=jnp.float32
    ).astype(jnp.bfloat16)
    spread = cut_exchange(modes, "freq", 2, 2, 0)
    table = gathered_copies(partner, "freq", 0)
    width = spread.shape[2]
    offset = lax.axis_index("freq") * width
    slice_weight = lax.dynamic_slice_in_dim(weight, offset, width, 0)
    freqs = jnp.arange(spread.shape[0], dtype=jnp.int32)
    source = (lax.axis_size("freq") - 1 - freqs // groups) * groups + table
    chosen = jnp.take(spread, source, axis=0)
    partial_value = cross_terms(spread, chosen, slice_weight, total)
    local = summed_on_arrival(partial_value.astype(jnp.bfloat16), "freq", 0)
    coherence = taken_together(local, "space")
    return (modes, energy, coherence)


def solution(mesh):
    in_specs = (P("freq", "space", None), P("space"), P("freq"), P("freq"))
    out_specs = (P("freq", None, "space"), P("freq", None), P("freq", None, None, None))
    return jax.shard_map(
        on_device, mesh=mesh, in_specs=in_specs, out_specs=out_specs, check_vma=False
    )
```

profile of v0, /device:TPU:1, one launch (start us, length us, event | category | flops | bytes accessed | tf_op | source)
XLA Modules:
  0.0 294.8 jit_solution(10261040301872561448)
XLA Ops:
  7.2 20.6 %fusion.2 = f32[16,256,256]{1,2,0:T(8,128)} fusion(bf16[16,3072,256]{2,1,0:T(8,128)(2,1)} %param.4, f32[3072]{0:T(1024)} %param.5), kind=kOutput, calls=%fused_computation.7 | convolution fusion | flops 6480199680 | bytes 29372416 | tf_op jit(solution)/shard_map/dot_general | solution.py:133
  27.8 4.0 %fusion.17 = (f32[16,128,128]{1,2,0:T(8,128)}, f32[16,128,128]{1,2,0:T(8,128)}) fusion(f32[16,256,256]{1,2,0:T(8,128)} %fusion.2), kind=kLoop, calls=%fused_computation.22 | loop fusion | flops 1048576 | bytes 6291456 | tf_op jit(solution)/shard_map/div | solution.py:100
  31.9 0.6 broadcast_in_dim.18
  32.4 8.2 %all-to-all-start.2 = ((s32[8,1,16]{2,1,0:T(1,128)}), s32[8,1,16]{2,1,0:T(1,128)S(1)}, u32[]{:S(2)}, u32[]{:S(2)}) async-start(s32[8,1,16]{2,1,0:T(1,128)} %broadcast_in_dim.18), calls=%async_computation.2 | async-start | bytes 8192 | tf_op jit(solution)/shard_map/all_to_all | solution.py:39
  40.6 118.2 %all-reduce.3.cloned.1.call-done = (f32[16,128,128]{1,2,0:T(8,128)}, f32[16,128,128]{1,2,0:T(8,128)}) async-done(((f32[16,128,128]{1,2,0:T(8,128)}, f32[16,128,128]{1,2,0:T(8,128)}), (f32[16,128,128]{1,2,0:T(8,128)}, f32[16,128,128]{1,2,0:T(8,128)})) %all-reduce.3.cloned.1.call-update) | async-done | bytes 2097168 | tf_op jit(solution)/shard_map/psum | solution.py:137
  158.8 1.3 neg.6
  160.2 4.1 %fusion.36 = f32[16,8,256]{2,1,0:T(8,128)S(1)} fusion(f32[8,256]{1,0:T(8,128)S(1)} %fusion.70, f32[16,128,128]{1,2,0:T(8,128)} %get-tuple-element.347, f32[16,128,128]{1,2,0:T(8,128)} %get-tuple-element.348, f32[16,128,128]{1,2,0:T(8,128)S(1)} %neg.6), kind=kOutput, calls=%fused_computation.80 | convolution fusion | flops 103809024 | bytes 3284992 | tf_op jit(solution)/shard_map/fkc,fdc->fkd/dot_general | solution.py:65
  165.1 0.3 add_reduce_fusion.96
  165.9 0.3 add_reduce_fusion.89
  167.5 0.3 add_reduce_fusion.87
  169.8 1.9 fusion.34
  172.6 0.3 add_reduce_fusion.68
  173.5 0.3 add_reduce_fusion.61
  175.0 0.3 add_reduce_fusion.59
  177.3 2.0 fusion.32
  180.1 0.3 add_reduce_fusion.40
  181.0 0.3 add_reduce_fusion.33
  182.5 0.3 add_reduce_fusion.31
  184.8 2.2 fusion.30
  187.8 0.3 add_reduce_fusion.12
  188.7 0.3 add_reduce_fusion.5
  192.6 2.0 fusion.28
  194.8 11.5 %convolution_convert_fusion = bf16[16,16,3072]{2,1,0:T(8,128)(2,1)S(1)} fusion(bf16[16,3072,256]{2,1,0:T(8,128)(2,1)} %param.4, bf16[16,16,256]{2,0,1:T(8,128)(2,1)S(1)} %pad_maximum_fusion.1), kind=kOutput, calls=%fused_computation.5 | convolution fusion | flops 403439616 | bytes 26869760 | tf_op jit(solution)/shard_map/fkc,fpc->fkp/dot_general | solution.py:140
  206.6 1.2 fusion.78
  207.8 18.6 %all_to_all.26 = bf16[8,8,16,384]{3,2,1,0:T(8,128)(2,1)S(1)} all-to-all(bf16[8,8,16,384]{3,2,1,0:T(8,128)(2,1)S(1)} %get-tuple-element.519), channel_id=1, replica_groups=mesh['freq'=8,'space'=16] {'freq'}, dimensions={0} | all-to-all | bytes 1572864 | tf_op jit(solution)/shard_map/all_to_all | solution.py:33
  226.4 3.8 %all-to-all-start.1 = ((bf16[8,8,16,384]{3,2,1,0:T(8,128)(2,1)}), bf16[8,8,16,384]{3,2,1,0:T(8,128)(2,1)S(1)}, u32[]{:S(2)}, u32[]{:S(2)}) async-start(bf16[8,8,16,384]{3,2,1,0:T(8,128)(2,1)} %get-tuple-element.520), calls=%async_computation.1 | async-start | bytes 1572864 | tf_op jit(solution)/shard_map/all_to_all | solution.py:33
  230.2 0.8 dynamic_slice.3
  231.1 0.5 broadcast.1034
  231.6 0.7 reduce.5
  232.4 7.7 %all-to-all-done.1 = bf16[8,8,16,384]{3,2,1,0:T(8,128)(2,1)S(1)} async-done(((bf16[8,8,16,384]{3,2,1,0:T(8,128)(2,1)}), bf16[8,8,16,384]{3,2,1,0:T(8,128)(2,1)S(1)}, u32[]{:S(2)}, u32[]{:S(2)}) %all-to-all-start.1) | async-done | bytes 786464 | tf_op jit(solution)/shard_map/all_to_all | solution.py:33
  240.2 1.1 copy-done
  241.4 0.4 convert_multiply_fusion
  241.8 3.3 %gather_fusion = bf16[128,16,384]{2,1,0:T(8,128)(2,1)} fusion(bf16[128,16,384]{2,1,0:T(8,128)(2,1)} %bitcast.180, s32[1024]{0:T(1024)S(1)} %pad_clamp_fusion), kind=kCustom, calls=%fused_computation | custom fusion | bytes 3146240 | tf_op jit(solution)/shard_map/jit(_take)/gather | solution.py:150
  245.1 1.7 broadcast_select_fusion
  246.8 1.6 fusion.5
  248.4 2.8 fusion.3
  251.2 2.4 fusion.11
  253.6 1.2 copy.89
  254.8 4.0 %fusion.14 = f32[128,8,8]{2,1,0:T(8,128)} fusion(f32[128,8,8]{2,1,0:T(8,128)} %fusion.3, f32[128,16,384]{2,1,0:T(8,128)S(1)} %convert_multiply_fusion, bf16[128,16,384]{2,1,0:T(8,128)(2,1)} %copy-done.1), kind=kOutput, calls=%fused_computation.20 | convolution fusion | flops 37756928 | bytes 2916352 | tf_op jit(solution)/shard_map/fkp,flp->fkl/dot_general | solution.py:121
  258.9 1.2 copy.90
  260.2 0.3 reshape.1905
  260.5 12.8 %all_to_all.27 = bf16[8,2,1024]{2,1,0:T(2,128)(2,1)S(1)} all-to-all(bf16[8,2,1024]{2,1,0:T(2,128)(2,1)S(1)} %reshape.1905), channel_id=1, replica_groups=mesh['freq'=8,'space'=16] {'freq'}, dimensions={0} | all-to-all | bytes 65536 | tf_op jit(solution)/shard_map/all_to_all | solution.py:50
  273.7 0.4 reshape.1907
  274.1 11.4 %all_to_all.28 = f32[16,1,2048]{2,1,0:T(1,128)S(1)} all-to-all(f32[16,1,2048]{2,1,0:T(1,128)S(1)} %reshape.1907), channel_id=1, replica_groups=mesh['freq'=8,'space'=16] {'space'}, dimensions={0} | all-to-all | bytes 262144 | tf_op jit(solution)/shard_map/all_to_all | solution.py:39
  285.4 0.5 broadcast.1035
  286.0 0.9 reduce.6
  286.9 0.4 reshape.1908
  287.3 0.7 bitcast_reduce_fusion
  (249 shorter events, 20.0 us)
Async XLA Ops:
  7.2 151.7 %all-reduce.3.cloned.1.call-start = ((), (), s32[]{:S(2)}) async-start(), calls=%async_computation.5 | async-start | bytes 4194304 | tf_op jit(solution)/shard_map/psum | solution.py:137
  27.8 4.0 %copy-start.5 = (s32[16]{0:T(128)S(1)}, s32[16]{0:T(128)}, u32[]{:S(2)}) copy-start(s32[16]{0:T(128)} %param.6) | copy-start | bytes 196
  32.4 175.3 %all-to-all-start.2 = ((s32[8,1,16]{2,1,0:T(1,128)}), s32[8,1,16]{2,1,0:T(1,128)S(1)}, u32[]{:S(2)}, u32[]{:S(2)}) async-start(s32[8,1,16]{2,1,0:T(1,128)} %broadcast_in_dim.18), calls=%async_computation.2 | async-start | bytes 8192 | tf_op jit(solution)/shard_map/all_to_all | solution.py:39
  160.1 9.6 %copy-start.3 = (f32[16,128,128]{1,2,0:T(8,128)S(1)}, f32[16,128,128]{1,2,0:T(8,128)}, u32[]{:S(2)}) copy-start(f32[16,128,128]{1,2,0:T(8,128)} %get-tuple-element.348) | copy-start | bytes 3145732
  160.2 9.7 %copy-start.7 = (f32[16,128,128]{1,2,0:T(8,128)S(1)}, f32[16,128,128]{1,2,0:T(8,128)}, u32[]{:S(2)}) copy-start(f32[16,128,128]{1,2,0:T(8,128)} %get-tuple-element.347) | copy-start | bytes 3145732
  190.8 3.9 %copy-start.6 = (s32[16]{0:T(128)S(1)}, s32[16]{0:T(128)}, u32[]{:S(2)}) copy-start(s32[16]{0:T(128)} %param.7) | copy-start | bytes 196
  194.7 11.7 %copy-start.4 = (f32[16,8]{0,1:T(8,128)}, f32[16,8]{0,1:T(8,128)S(1)}, u32[]{:S(2)}) copy-start(f32[16,8]{0,1:T(8,128)S(1)} %fusion.27) | copy-start | bytes 1540
  206.4 20.0 %copy-start.2 = (bf16[16,16,3072]{2,1,0:T(8,128)(2,1)}, bf16[16,16,3072]{2,1,0:T(8,128)(2,1)S(1)}, u32[]{:S(2)}) copy-start(bf16[16,16,3072]{2,1,0:T(8,128)(2,1)S(1)} %convolution_convert_fusion) | copy-start | bytes 4718596
  226.4 13.7 %all-to-all-start.1 = ((bf16[8,8,16,384]{3,2,1,0:T(8,128)(2,1)}), bf16[8,8,16,384]{3,2,1,0:T(8,128)(2,1)S(1)}, u32[]{:S(2)}, u32[]{:S(2)}) async-start(bf16[8,8,16,384]{3,2,1,0:T(8,128)(2,1)} %get-tuple-element.520), calls=%async_computation.1 | async-start | bytes 1572864 | tf_op jit(solution)/shard_map/all_to_all | solution.py:33
  240.2 1.2 copy-start
  246.8 6.8 %copy-start.1 = (bf16[128,16,384]{2,1,0:T(8,128)(2,1)}, bf16[128,16,384]{2,1,0:T(8,128)(2,1)S(1)}, u32[]{:S(2)}) copy-start(bf16[128,16,384]{2,1,0:T(8,128)(2,1)S(1)} %broadcast_select_fusion) | copy-start | bytes 4718596
Sparse Core Ops, SparseCore 0:
  32.0 126.8 all-reduce.2
where the time goes:
time: 295 us
  waiting for transfers between devices  126 us (43%)
  matrix products  55.1 us (19%)
  blocking collectives  42.8 us (15%)
  other arithmetic  31.6 us (11%)
  between operations  14.7 us (5%)
  local copies, waits for them, and re-layouts  12.8 us (4%)
  starting transfers between devices  12 us (4%)
    psum x1, waiting for transfers between devices, on_device(): gram_re, gram_im = lax.psum((local_re, local_im), 'space')  118 us
    dot_general x1, matrix products, on_device(): lax.dot_general(spectra, weighted, (((1,), (1,)), ((0,), (0,))), preferre...  20.6 us
    all_to_all x1, blocking collectives, cut_exchange(): lax.all_to_all(share, axis, split_axis=0, concat_axis=0, tiled=True)  18.6 us
    all_to_all x1, blocking collectives, summed_on_arrival(): parts = lax.all_to_all(cut_along(array, dim, size), axis, 0, 0, tiled=True)  12.8 us
    dot_general x5, matrix products, apply_operator(): jnp.einsum('fkc,fdc->fkd', basis, operator, precision=lax.Precision.HIGHEST)  12.1 us
    dot_general x1, matrix products, on_device(): jnp.einsum('fkc,fpc->fkp', coefficient, spectra, preferred_element_type=j...  11.5 us
    all_to_all x1, blocking collectives, copy_for_each(): lax.all_to_all(jnp.broadcast_to(array[None], (size, *array.shape)), axis,...  11.4 us
    dot_general x4, matrix products, inner(): return jnp.einsum('fkp,flp->fkl', left, right, precision=highest)  10.8 us
  transfers between devices with their start and end apart: 3, of which 2 were waited for; matrix products, arithmetic and copies ran while one was open for 17% of the time, Pallas kernels for 0%

commit v1 on v0

v1 whole, which is shorter than its diff:
```python
import functools

import jax
import jax.numpy as jnp
from jax import lax
from jax.experimental import pallas as pl
from jax.experimental.pallas import tpu as pltpu
from jax.sharding import PartitionSpec as P

KMAX = 8
ITERS = 4
EPS = 1e-06
AHEAD = 4
MESH = pl.DeviceIdType.MESH
HIGHEST = lax.Precision.HIGHEST


def moment(spectra, weighted):
    return lax.dot_general(
        spectra, weighted, (((0,), (0,)), ((), ())), preferred_element_type=jnp.float32
    )


def times_transposed(left, right):
    return lax.dot_general(
        left, right, (((1,), (1,)), ((), ())), preferred_element_type=jnp.float32
    )


def triangles(half):
    row = lax.broadcasted_iota(jnp.int32, (half, half), 0)
    col = lax.broadcasted_iota(jnp.int32, (half, half), 1)
    return row, col


def packed(moments):
    half = moments.shape[0] // 2
    row, col = triangles(half)
    gram_re = moments[:half, :half] + moments[half:, half:]
    gram_im = moments[:half, half:] - moments[half:, :half]
    return jnp.where(row <= col, gram_re, gram_im)


def unpacked(square, total):
    row, col = triangles(square.shape[0])
    flipped = square.T
    gram_re = jnp.where(row <= col, square, flipped)
    gram_im = jnp.where(row > col, square, jnp.where(row < col, -flipped, 0.0))
    return gram_re / total, gram_im / total


def orthonormal(vec_re, vec_im):
    ranks = lax.broadcasted_iota(jnp.int32, vec_re.shape, 0)
    for k in range(KMAX):
        own_re = jnp.broadcast_to(vec_re[k : k + 1], vec_re.shape)
        own_im = jnp.broadcast_to(vec_im[k : k + 1], vec_im.shape)
        norm = jnp.sum(own_re * own_re + own_im * own_im, axis=1, keepdims=True)
        proj_re = jnp.sum(own_re * vec_re + own_im * vec_im, axis=1, keepdims=True)
        proj_im = jnp.sum(own_re * vec_im - own_im * vec_re, axis=1, keepdims=True)
        inverse = 1.0 / jnp.sqrt(norm + EPS)
        unit_re, unit_im = own_re * inverse, own_im * inverse
        proj_re, proj_im = proj_re * inverse, proj_im * inverse
        new_re = vec_re - proj_re * unit_re + proj_im * unit_im
        new_im = vec_im - proj_re * unit_im - proj_im * unit_re
        vec_re = jnp.where(ranks > k, new_re, jnp.where(ranks == k, unit_re, vec_re))
        vec_im = jnp.where(ranks > k, new_im, jnp.where(ranks == k, unit_im, vec_im))
    return vec_re, vec_im


def solved(gram_re, gram_im, count):
    half = gram_re.shape[0]
    operator = jnp.concatenate([gram_re, gram_im], axis=1)

    def applied(vec_re, vec_im):
        both = jnp.concatenate([vec_re, vec_im], axis=0)
        image = jnp.dot(both, operator, precision=HIGHEST, preferred_element_type=jnp.float32)
        return (
            image[:KMAX, :half] + image[KMAX:, half:],
            image[KMAX:, :half] - image[:KMAX, half:],
        )

    vec_re, vec_im = orthonormal(gram_re[:KMAX], -gram_im[:KMAX])
    for _ in range(ITERS - 1):
        vec_re, vec_im = orthonormal(*applied(vec_re, vec_im))
    image_re, image_im = applied(vec_re, vec_im)
    energy = jnp.sum(vec_re * image_re + vec_im * image_im, axis=1, keepdims=True)
    ranks = lax.broadcasted_iota(jnp.int32, (KMAX, 1), 0)
    scale = jnp.where(ranks < count, 1.0 / jnp.sqrt(energy + EPS), 0.0)
    part_re, part_im = vec_re * scale, vec_im * scale
    coefficient = jnp.concatenate(
        [
            jnp.concatenate([part_re, -part_im], axis=1),
            jnp.concatenate([part_im, part_re], axis=1),
        ],
        axis=0,
    )
    return coefficient.astype(jnp.bfloat16), energy


def kernel(
    n_freq,
    n_space,
    total,
    spectra_hbm,
    weight_ref,
    partner_ref,
    counts_ref,
    modes_hbm,
    energy_ref,
    coherence_ref,
    spectra,
    column,
    weighted,
    squares,
    from_core,
    from_chips,
    coef_own,
    coefs,
    energy_own,
    energies,
    modes,
    arrived,
    weight_rows,
    weight_in,
    partner_row,
    partner_in,
    parts,
    parts_in,
    sums,
    load_sem,
    store_sem,
    core_send,
    core_recv,
    chip_send,
    chip_recv,
    coef_send,
    coef_recv,
    energy_send,
    energy_recv,
    mode_send,
    mode_recv,
    weight_sem,
    row_send,
    row_recv,
    part_send,
    part_recv,
    sum_send,
    sum_recv,
):
    freqs, points, wide = spectra.shape
    quarter = points // 4
    g, s = lax.axis_index("freq"), lax.axis_index("space")
    core, chip = lax.rem(s, 2), s // 2
    n_chips = n_space // 2
    n_y = max(n_chips // 2, 1)
    z_lo, y = chip // n_y, lax.rem(chip, n_y)
    x, z_hi = g // 2, lax.rem(g, 2)
    n_x = n_freq // 2

    def remote(src, dst, send, recv, device):
        return pltpu.make_async_remote_copy(
            src_ref=src,
            dst_ref=dst,
            send_sem=send,
            recv_sem=recv,
            device_id=device,
            device_id_type=MESH,
        )

    def space_peer(offset):
        return (g, lax.rem(s + offset, n_space))

    other_s = lax.rem(s + n_space // 2, n_space)

    def meeting(slot):
        to_x = x if slot < 2 else n_x - 1 - x
        to_z = z_hi if slot % 2 == 0 else 1 - z_hi
        part = 2 * to_z + (2 * to_x) // n_x
        return (2 * to_x + to_z, other_s), part

    def chip_at(step):
        ahead = n_chips - 1 - step
        to_z = lax.rem(z_lo + ahead // n_y, 2)
        to_y = lax.rem(y + lax.rem(ahead, n_y), n_y)
        return to_z * n_y + to_y

    def freq_at(step):
        first = step < n_chips
        place = jnp.where(first, step, step - n_chips)
        return 2 * chip_at(place) + jnp.where(first, 1 - core, core)

    def load(step):
        freq = freq_at(step)
        return pltpu.make_async_copy(spectra_hbm.at[freq], spectra.at[freq], load_sem.at[freq])

    for step in range(min(AHEAD, freqs)):
        load(step).start()

    barrier = pltpu.get_barrier_semaphore()
    for offset in range(1, n_space):
        pl.semaphore_signal(barrier, inc=1, device_id=space_peer(offset), device_id_type=MESH)
    for slot in range(1, 4):
        pl.semaphore_signal(barrier, inc=1, device_id=meeting(slot)[0], device_id_type=MESH)

    tiles = points // 128
    for tile in range(tiles):
        line = weight_ref[tile : tile + 1, :]
        column[tile * 128 : (tile + 1) * 128, :] = jnp.broadcast_to(line, (128, 128)).T
        place, within = tile // (tiles // 4), tile % (tiles // 4)
        weight_rows[place, :, within * 128 : (within + 1) * 128] = line
    lanes = partner_row.shape[1]
    which = lax.broadcasted_iota(jnp.int32, (1, lanes), 1) // (2 * KMAX)
    row = jnp.zeros((1, lanes), jnp.float32)
    for freq in range(freqs):
        row = jnp.where(which == freq, partner_ref[freq].astype(jnp.float32), row)
    partner_row[...] = row

    pl.semaphore_wait(barrier, n_space - 1 + 3)

    def core_copy(step):
        return remote(
            squares.at[step],
            from_core.at[step],
            core_send.at[step],
            core_recv.at[step],
            (g, s + 1 - 2 * core),
        )

    def chip_copy(step):
        return remote(
            squares.at[n_chips + step],
            from_chips.at[step],
            chip_send.at[step],
            chip_recv.at[step],
            (g, 2 * chip_at(step) + core),
        )

    def gram(step):
        freq = freq_at(step)
        load(step).wait()

        @pl.when(step + AHEAD < freqs)
        def _():
            load(step + AHEAD).start()

        rows = 256 if points % 256 == 0 else 128
        for start in range(0, points, rows):
            block = spectra[freq, start : start + rows, :].astype(jnp.float32)
            scale = column[start : start + rows, :]
            scale = jnp.concatenate([scale, scale], axis=1)
            weighted[start : start + rows, :] = (block * scale).astype(jnp.bfloat16)
        return packed(moment(spectra[freq], weighted[...]))

    @pl.loop(0, n_chips)
    def _(step):
        @pl.when(step >= 1)
        def _():
            core_copy(step - 1).start()

        squares[step] = gram(step)

    @pl.loop(0, n_chips)
    def _(step):
        @pl.when(step == 0)
        def _():
            core_copy(n_chips - 1).start()

        @pl.when(step >= 1)
        def _():
            chip_copy(step - 1).start()

        square = gram(n_chips + step)
        core_copy(step).wait_recv()
        squares[n_chips + step] = square + from_core[step]

    weight_copy = remote(
        weight_rows.at[meeting(0)[1]], weight_in, weight_sem.at[0], weight_sem.at[1], meeting(0)[0]
    )
    weight_copy.start()
    row_copies = [
        remote(
            partner_row, partner_in.at[slot], row_send.at[slot], row_recv.at[slot], meeting(slot)[0]
        )
        for slot in range(4)
    ]
    for copy in row_copies:
        copy.start()

    square = squares[2 * n_chips - 1]
    for step in range(n_chips - 1):
        chip_copy(step).wait_recv()
        square = square + from_chips[step]
    coefficient, energy = solved(*unpacked(square, total), counts_ref[s])
    coef_own[...] = coefficient
    energy_own[...] = jnp.broadcast_to(energy, energy_own.shape)
    coefs[s] = coefficient
    energies[s] = jnp.broadcast_to(energy, energy_own.shape)

    coef_copies, energy_copies, sum_copies = [], [], []
    for offset in range(1, n_space):
        peer = space_peer(offset)
        send, recv = coef_send.at[offset], coef_recv.at[offset]
        coef_copies.append(remote(coef_own, coefs.at[s], send, recv, peer))
        send, recv = energy_send.at[offset], energy_recv.at[offset]
        energy_copies.append(remote(energy_own, energies.at[s], send, recv, peer))
        send, recv = sum_send.at[offset], sum_recv.at[offset]
        sum_copies.append(remote(sums.at[s], sums.at[s], send, recv, peer))
    for copy in coef_copies:
        copy.start()
    for copy in energy_copies:
        copy.start()
    for copy in coef_copies:
        copy.wait_recv()

    def mode_copy(freq, slot):
        device, part = meeting(slot)
        start = pl.multiple_of(part * quarter, 128)
        return remote(
            modes.at[freq, :, pl.ds(start, quarter)],
            arrived.at[slot, freq],
            mode_send.at[slot, freq],
            mode_recv.at[slot, freq],
            device,
        )

    def mode_store(freq):
        return pltpu.make_async_copy(modes.at[freq], modes_hbm.at[freq], store_sem.at[freq])

    @pl.loop(0, freqs)
    def _(freq):
        modes[freq] = times_transposed(coefs[freq], spectra[freq]).astype(jnp.bfloat16)
        for slot in range(4):
            mode_copy(freq, slot).start()
        mode_store(freq).start()

    for copy in row_copies:
        copy.wait_recv()
    weight_copy.wait_recv()

    @pl.loop(0, freqs)
    def _(freq):
        for slot in range(4):
            mode_copy(freq, slot).wait_recv()

    rows = 2 * KMAX * freqs
    owner = lax.broadcasted_iota(jnp.int32, (rows, rows), 0) // (2 * KMAX)
    owner = owner.astype(jnp.float32)
    is_re = lax.rem(lax.broadcasted_iota(jnp.int32, (KMAX, rows), 1), 2 * KMAX) < KMAX
    line = weight_in[...]
    part_copies = []
    for slot in range(4):
        phi = arrived[slot].reshape(rows, quarter)
        psi = arrived[3 - slot].reshape(rows, quarter)
        wpsi = (psi.astype(jnp.float32) * line).astype(jnp.bfloat16)
        cross = times_transposed(wpsi, phi)
        cross = jnp.where(owner == partner_in[slot], cross, 0.0)
        chosen = jnp.sum(cross.reshape(freqs, 2 * KMAX, rows), axis=0)
        low, high = chosen[:KMAX], chosen[KMAX:]
        parts[slot] = jnp.where(
            is_re,
            low + pltpu.roll(high, rows - KMAX, 1),
            pltpu.roll(high, KMAX, 1) - low,
        )
        copy = remote(
            parts.at[slot],
            parts_in.at[slot],
            part_send.at[slot],
            part_recv.at[slot],
            meeting(slot)[0],
        )
        copy.start()
        part_copies.append(copy)
    for copy in part_copies:
        copy.wait_recv()
    sums[s] = (parts_in[0] + parts_in[1]) + (parts_in[2] + parts_in[3])
    for copy in sum_copies:
        copy.start()
    for copy in energy_copies:
        copy.wait_recv()
    energy_ref[...] = energies[...]
    for copy in sum_copies:
        copy.wait_recv()
    whole = sums[0]
    for place in range(1, n_space):
        whole = whole + sums[place]
    coherence_ref[...] = whole / total

    @pl.loop(0, n_chips)
    def _(step):
        core_copy(step).wait_send()

    @pl.loop(0, n_chips - 1)
    def _(step):
        chip_copy(step).wait_send()

    @pl.loop(0, freqs)
    def _(freq):
        for slot in range(4):
            mode_copy(freq, slot).wait_send()
        mode_store(freq).wait()

    sends = row_copies + coef_copies + energy_copies + part_copies + sum_copies
    for copy in [weight_copy] + sends:
        copy.wait_send()


def on_device(n_freq, n_space, spectra, weight, partner, counts):
    freqs, points, wide = spectra.shape
    half = wide // 2
    rows = 2 * KMAX
    lanes = rows * freqs
    quarter = points // 4
    n_chips = n_space // 2
    f32, bf16 = jnp.float32, jnp.bfloat16
    dma = pltpu.SemaphoreType.DMA
    vmem, smem = pltpu.VMEM, pltpu.SMEM
    modes, energy, coherence = pl.pallas_call(
        functools.partial(kernel, n_freq, n_space, points * n_space),
        out_shape=(
            jax.ShapeDtypeStruct((freqs, rows, points), bf16),
            jax.ShapeDtypeStruct((freqs, KMAX, 128), f32),
            jax.ShapeDtypeStruct((KMAX, lanes), f32),
        ),
        in_specs=[
            pl.BlockSpec(memory_space=pl.ANY),
            pl.BlockSpec(memory_space=vmem),
            pl.BlockSpec(memory_space=smem),
            pl.BlockSpec(memory_space=smem),
        ],
        out_specs=(
            pl.BlockSpec(memory_space=pl.ANY),
            pl.BlockSpec(memory_space=vmem),
            pl.BlockSpec(memory_space=vmem),
        ),
        scratch_shapes=[
            vmem((freqs, points, wide), bf16),
            vmem((points, 128), f32),
            vmem((points, wide), bf16),
            vmem((2 * n_chips, half, half), f32),
            vmem((n_chips, half, half), f32),
            vmem((n_chips, half, half), f32),
            vmem((rows, wide), bf16),
            vmem((freqs, rows, wide), bf16),
            vmem((KMAX, 128), f32),
            vmem((freqs, KMAX, 128), f32),
            vmem((freqs, rows, points), bf16),
            vmem((4, freqs, rows, quarter), bf16),
            vmem((4, 1, quarter), f32),
            vmem((1, quarter), f32),
            vmem((1, lanes), f32),
            vmem((4, 1, lanes), f32),
            vmem((4, KMAX, lanes), f32),
            vmem((4, KMAX, lanes), f32),
            vmem((n_space, KMAX, lanes), f32),
            dma((freqs,)),
            dma((freqs,)),
            dma((n_chips,)),
            dma((n_chips,)),
            dma((n_chips,)),
            dma((n_chips,)),
            dma((n_space,)),
            dma((n_space,)),
            dma((n_space,)),
            dma((n_space,)),
            dma((4, freqs)),
            dma((4, freqs)),
            dma((2,)),
            dma((4,)),
            dma((4,)),
            dma((4,)),
            dma((4,)),
            dma((n_space,)),
            dma((n_space,)),
        ],
        compiler_params=pltpu.CompilerParams(
            collective_id=0, has_side_effects=True, vmem_limit_bytes=60 * 1024 * 1024
        ),
    )(spectra, weight.reshape(points // 128, 128), partner, counts)
    coherence = coherence.reshape(KMAX, freqs, 2, KMAX).transpose(1, 2, 3, 0)
    return modes, energy[:, :, 0], coherence


def solution(mesh):
    in_specs = (P("freq", "space", None), P("space"), P("freq"), P("freq"))
    out_specs = (P("freq", None, "space"), P("freq", None), P("freq", None, None, None))
    body = functools.partial(on_device, mesh.shape["freq"], mesh.shape["space"])
    return jax.shard_map(
        body, mesh=mesh, in_specs=in_specs, out_specs=out_specs, check_vma=False
    )
```

time: 295 us -> 73.8 us (0.25)
  waiting for transfers between devices: 126 us -> 0 us
  Pallas kernels: 0 us -> 67 us
  matrix products: 55.1 us -> 0 us
  blocking collectives: 42.8 us -> 0 us
  other arithmetic: 31.6 us -> 0 us
  between operations: 14.7 us -> 0.65 us
  starting transfers between devices: 12 us -> 0 us
  local copies, waits for them, and re-layouts: 12.8 us -> 5.9 us
    psum x1 -> x0, waiting for transfers between devices: 118 us -> none  [on_device(): gram_re, gram_im = lax.psum((local_re, local_im), 'space')]
    pallas_call x0 -> x1, Pallas kernels: none -> 67 us  [on_device(): pl.pallas_call(functools.partial(kernel, n_freq, n_space, points * n_spac...]
    dot_general x11 -> x0, matrix products: 55.1 us -> none  [the longest x1 20.6 us: on_device(): lax.dot_general(spectra, weighted, (((1,), (1,)), ((0,), (0,))), preferre...]
    all_to_all x3 -> x0, blocking collectives: 42.8 us -> none  [the longest x1 18.6 us: cut_exchange(): lax.all_to_all(share, axis, split_axis=0, concat_axis=0, tiled=True)]
    reduce_sum x79 -> x0, other arithmetic: 15.2 us -> none  [the longest x44 10.6 us: orthonormal(): jnp.sum(early_re * vec_re + early_im * vec_im, axis=1, keepdims=True)]
    all_to_all x2 -> x0, starting transfers between devices: 12 us -> none  [the longest x1 8.15 us: copy_for_each(): lax.all_to_all(jnp.broadcast_to(array[None], (size, *array.shape)), axis,...]
    all_to_all x2 -> x0, waiting for transfers between devices: 7.68 us -> none  [the longest x1 7.68 us: cut_exchange(): lax.all_to_all(share, axis, split_axis=0, concat_axis=0, tiled=True)]
    div x29 -> x0, other arithmetic: 6.17 us -> none  [the longest x1 3.99 us: combine(): gram_im = (moments[:, :half, half:] - moments[:, half:, :half]) / total]
  transfers between devices with their start and end apart: 3 -> 0, of which waited for: 2 -> 0; matrix products, arithmetic and copies ran while one was open for 17% -> 0% of each run, Pallas kernels for 0% -> 0%
where the time goes in v1:
time: 73.8 us; the launch traced here: 73.6 us
  Pallas kernels  67 us (91%)
  local copies, waits for them, and re-layouts  5.9 us (8%)
    pallas_call x1, Pallas kernels, on_device(): pl.pallas_call(functools.partial(kernel, n_freq, n_space, points * n_spac...  67 us
    unnamed x2, local copies, waits for them, and re-layouts  3.43 us
    slice x1, local copies, waits for them, and re-layouts, on_device(): return (modes, energy[:, :, 0], coherence)  1.55 us

profile of v1, /device:TPU:1, one launch (start us, length us, event | category | flops | bytes accessed | tf_op | source)
XLA Modules:
  0.0 73.6 jit_solution(8371509285380261691)
XLA Ops:
  0.6 67.0 %shard_map.67 = (bf16[16,16,3072]{2,1,0:T(8,128)(2,1)}, f32[16,8,128]{2,1,0:T(8,128)}, f32[8,256]{1,0:T(8,128)}) custom-call(bf16[16,3072,256]{2,1,0:T(8,128)(2,1)} %spectra_hbm.1, f32[24,128]{1,0:T(8,128)} %bitcast.6, s32[16]{0:T(128)} %partner_ref.1, s32[16]{0:T(128)} %counts_ref.1), custom_call_target="tpu_custom_call" | custom-call | tf_op jit(solution)/shard_map/pallas_call | solution.py:417
  67.7 1.5 %copy.9 = f32[16,8,1]{0,1,2:T(8,128)} copy(f32[16,8,1]{2,1,0:T(8,128)} %bitcast.5) | data formatting | bytes 1024 | tf_op jit(solution)/shard_map/slice | solution.py:480
  69.2 0.9 %reshape.13 = f32[8,16,2,8]{3,2,1,0:T(2,128)S(1)} reshape(f32[8,256]{1,0:T(8,128)} %get-tuple-element.8) | data formatting | bytes 16384 | tf_op jit(solution)/shard_map/reshape | solution.py:479
  70.1 0.7 %copy.10 = f32[16,2,8,8]{0,3,2,1:T(8,128)} copy(f32[16,2,8,8]{2,1,0,3:T(2,128)S(1)} %bitcast.4) | data formatting | bytes 16384
  70.9 2.7 %copy.12 = bf16[16,16,3072]{2,1,0:T(8,128)(2,1)} copy(bf16[16,16,3072]{2,1,0:T(8,128)(2,1)} %get-tuple-element.15) | data formatting | bytes 3145728

commit v2 on v1

--- a/solution.py
+++ b/solution.py
@@ -10,15 +10,14 @@
 KMAX = 8
 ITERS = 4
 EPS = 1e-06
-AHEAD = 4
+AHEAD = 5
 MESH = pl.DeviceIdType.MESH
 HIGHEST = lax.Precision.HIGHEST
 
 
-def moment(spectra, weighted):
-    return lax.dot_general(
-        spectra, weighted, (((0,), (0,)), ((), ())), preferred_element_type=jnp.float32
-    )
+def moment(spectra, weight):
+    turned = spectra.T.astype(jnp.float32) * weight
+    return jnp.dot(turned.astype(jnp.bfloat16), spectra, preferred_element_type=jnp.float32)
 
 
 def times_transposed(left, right):
@@ -57,7 +56,7 @@
         norm = jnp.sum(own_re * own_re + own_im * own_im, axis=1, keepdims=True)
         proj_re = jnp.sum(own_re * vec_re + own_im * vec_im, axis=1, keepdims=True)
         proj_im = jnp.sum(own_re * vec_im - own_im * vec_re, axis=1, keepdims=True)
-        inverse = 1.0 / jnp.sqrt(norm + EPS)
+        inverse = lax.rsqrt(norm + EPS)
         unit_re, unit_im = own_re * inverse, own_im * inverse
         proj_re, proj_im = proj_re * inverse, proj_im * inverse
         new_re = vec_re - proj_re * unit_re + proj_im * unit_im
@@ -85,7 +84,7 @@
     image_re, image_im = applied(vec_re, vec_im)
     energy = jnp.sum(vec_re * image_re + vec_im * image_im, axis=1, keepdims=True)
     ranks = lax.broadcasted_iota(jnp.int32, (KMAX, 1), 0)
-    scale = jnp.where(ranks < count, 1.0 / jnp.sqrt(energy + EPS), 0.0)
+    scale = jnp.where(ranks < count, lax.rsqrt(energy + EPS), 0.0)
     part_re, part_im = vec_re * scale, vec_im * scale
     coefficient = jnp.concatenate(
         [
@@ -109,8 +108,6 @@
     energy_ref,
     coherence_ref,
     spectra,
-    column,
-    weighted,
     squares,
     from_core,
     from_chips,
@@ -120,7 +117,7 @@
     energies,
     modes,
     arrived,
-    weight_rows,
+    weight_row,
     weight_in,
     partner_row,
     partner_in,
@@ -178,15 +175,24 @@
         part = 2 * to_z + (2 * to_x) // n_x
         return (2 * to_x + to_z, other_s), part
 
-    def chip_at(step):
-        ahead = n_chips - 1 - step
+    def chip_ahead(ahead):
         to_z = lax.rem(z_lo + ahead // n_y, 2)
         to_y = lax.rem(y + lax.rem(ahead, n_y), n_y)
         return to_z * n_y + to_y
 
+    def chip_at(step):
+        return chip_ahead(n_chips - 1 - step)
+
+    def slot_at(step):
+        pair, second = step // 2, lax.rem(step, 2) == 1
+        early = jnp.where(pair == 0, 0, n_chips + pair - 1)
+        late = jnp.where(pair == n_chips - 1, 2 * n_chips - 1, pair + 1)
+        return jnp.where(second, late, early)
+
     def freq_at(step):
-        first = step < n_chips
-        place = jnp.where(first, step, step - n_chips)
+        slot = slot_at(step)
+        first = slot < n_chips
+        place = jnp.where(first, slot, slot - n_chips)
         return 2 * chip_at(place) + jnp.where(first, 1 - core, core)
 
     def load(step):
@@ -202,20 +208,14 @@
     for slot in range(1, 4):
         pl.semaphore_signal(barrier, inc=1, device_id=meeting(slot)[0], device_id_type=MESH)
 
-    tiles = points // 128
-    for tile in range(tiles):
-        line = weight_ref[tile : tile + 1, :]
-        column[tile * 128 : (tile + 1) * 128, :] = jnp.broadcast_to(line, (128, 128)).T
-        place, within = tile // (tiles // 4), tile % (tiles // 4)
-        weight_rows[place, :, within * 128 : (within + 1) * 128] = line
+    for tile in range(points // 128):
+        weight_row[:, tile * 128 : (tile + 1) * 128] = weight_ref[tile : tile + 1, :]
     lanes = partner_row.shape[1]
     which = lax.broadcasted_iota(jnp.int32, (1, lanes), 1) // (2 * KMAX)
     row = jnp.zeros((1, lanes), jnp.float32)
     for freq in range(freqs):
         row = jnp.where(which == freq, partner_ref[freq].astype(jnp.float32), row)
     partner_row[...] = row
-
-    pl.semaphore_wait(barrier, n_space - 1 + 3)
 
     def core_copy(step):
         return remote(
@@ -235,82 +235,88 @@
             (g, 2 * chip_at(step) + core),
         )
 
-    def gram(step):
-        freq = freq_at(step)
-        load(step).wait()
-
-        @pl.when(step + AHEAD < freqs)
-        def _():
-            load(step + AHEAD).start()
-
-        rows = 256 if points % 256 == 0 else 128
-        for start in range(0, points, rows):
-            block = spectra[freq, start : start + rows, :].astype(jnp.float32)
-            scale = column[start : start + rows, :]
-            scale = jnp.concatenate([scale, scale], axis=1)
-            weighted[start : start + rows, :] = (block * scale).astype(jnp.bfloat16)
-        return packed(moment(spectra[freq], weighted[...]))
-
-    @pl.loop(0, n_chips)
-    def _(step):
-        @pl.when(step >= 1)
-        def _():
-            core_copy(step - 1).start()
-
-        squares[step] = gram(step)
-
-    @pl.loop(0, n_chips)
-    def _(step):
-        @pl.when(step == 0)
-        def _():
-            core_copy(n_chips - 1).start()
-
-        @pl.when(step >= 1)
-        def _():
-            chip_copy(step - 1).start()
-
-        square = gram(n_chips + step)
-        core_copy(step).wait_recv()
-        squares[n_chips + step] = square + from_core[step]
-
+    def gram(*steps):
+        for step in steps:
+            load(step).wait()
+
+            @pl.when(step + AHEAD < freqs)
+            def _():
+                load(step + AHEAD).start()
+
+        for step in steps:
+            squares[slot_at(step)] = packed(moment(spectra[freq_at(step)], weight_row[...]))
+
+    def add_and_send(k):
+        core_copy(k).wait_recv()
+        squares[n_chips + k] = squares[n_chips + k] + from_core[k]
+        chip_copy(k).start()
+
+    gram(0, 1)
+    pl.semaphore_wait(barrier, n_space - 1 + 3)
+    core_copy(0).start()
+    core_copy(1).start()
+
+    @pl.loop(1, n_chips - 1)
+    def _(pair):
+        gram(2 * pair, 2 * pair + 1)
+        core_copy(pair + 1).start()
+        add_and_send(pair - 1)
+
+    gram(2 * n_chips - 2)
+    add_and_send(n_chips - 2)
+
+    start = pl.multiple_of(meeting(0)[1] * quarter, 128)
     weight_copy = remote(
-        weight_rows.at[meeting(0)[1]], weight_in, weight_sem.at[0], weight_sem.at[1], meeting(0)[0]
+        weight_row.at[:, pl.ds(start, quarter)],
+        weight_in,
+        weight_sem.at[0],
+        weight_sem.at[1],
+        meeting(0)[0],
     )
-    weight_copy.start()
     row_copies = [
         remote(
             partner_row, partner_in.at[slot], row_send.at[slot], row_recv.at[slot], meeting(slot)[0]
         )
         for slot in range(4)
     ]
+    weight_copy.start()
     for copy in row_copies:
         copy.start()
 
-    square = squares[2 * n_chips - 1]
+    gram(2 * n_chips - 1)
+    core_copy(n_chips - 1).wait_recv()
+    square = squares[2 * n_chips - 1] + from_core[n_chips - 1]
     for step in range(n_chips - 1):
         chip_copy(step).wait_recv()
         square = square + from_chips[step]
     coefficient, energy = solved(*unpacked(square, total), counts_ref[s])
     coef_own[...] = coefficient
-    energy_own[...] = jnp.broadcast_to(energy, energy_own.shape)
     coefs[s] = coefficient
-    energies[s] = jnp.broadcast_to(energy, energy_own.shape)
+    ranks = lax.broadcasted_iota(jnp.int32, (KMAX, 128), 0)
+    lane = lax.broadcasted_iota(jnp.int32, (KMAX, 128), 1)
+    energy = jnp.sum(jnp.where(ranks == lane, energy, 0.0), axis=0, keepdims=True)
+    energy_own[...] = energy
+    energies[s] = energy
+
+    near = [ahead for ahead in (0, 1, 3, 4, 2, 5, 7, 6) if ahead < n_chips]
+    peers = [2 * chip_ahead(ahead) + lax.rem(core + flip, 2) for ahead in near for flip in (0, 1)]
+    peers = peers[1:]
+
+    def coef_copy(peer, owner):
+        send, recv = coef_send.at[peer], coef_recv.at[owner]
+        return remote(coef_own, coefs.at[owner], send, recv, (g, peer))
 
     coef_copies, energy_copies, sum_copies = [], [], []
-    for offset in range(1, n_space):
-        peer = space_peer(offset)
-        send, recv = coef_send.at[offset], coef_recv.at[offset]
-        coef_copies.append(remote(coef_own, coefs.at[s], send, recv, peer))
-        send, recv = energy_send.at[offset], energy_recv.at[offset]
-        energy_copies.append(remote(energy_own, energies.at[s], send, recv, peer))
-        send, recv = sum_send.at[offset], sum_recv.at[offset]
-        sum_copies.append(remote(sums.at[s], sums.at[s], send, recv, peer))
+    for peer in peers:
+        coef_copies.append(coef_copy(peer, s))
+        send, recv = energy_send.at[peer], energy_recv.at[s]
+        energy_copies.append(remote(energy_own, energies.at[s], send, recv, (g, peer)))
+        send, recv = sum_send.at[peer], sum_recv.at[s]
+        sum_copies.append(remote(sums.at[s], sums.at[s], send, recv, (g, peer)))
     for copy in coef_copies:
         copy.start()
     for copy in energy_copies:
         copy.start()
-    for copy in coef_copies:
-        copy.wait_recv()
 
     def mode_copy(freq, slot):
         device, part = meeting(slot)
@@ -327,9 +333,18 @@
         return pltpu.make_async_copy(modes.at[freq], modes_hbm.at[freq], store_sem.at[freq])
 
     @pl.loop(0, freqs)
-    def _(freq):
+    def _(step):
+        ahead = jnp.int32(near[0])
+        for place in range(1, n_chips):
+            ahead = jnp.where(step // 2 == place, near[place], ahead)
+        freq = 2 * chip_ahead(ahead) + lax.rem(core + step, 2)
+
+        @pl.when(step > 0)
+        def _():
+            coef_copy(freq, freq).wait_recv()
+
         modes[freq] = times_transposed(coefs[freq], spectra[freq]).astype(jnp.bfloat16)
-        for slot in range(4):
+        for slot in (2, 3, 0, 1):
             mode_copy(freq, slot).start()
         mode_store(freq).start()
 
@@ -375,15 +390,32 @@
     sums[s] = (parts_in[0] + parts_in[1]) + (parts_in[2] + parts_in[3])
     for copy in sum_copies:
         copy.start()
-    for copy in energy_copies:
-        copy.wait_recv()
-    energy_ref[...] = energies[...]
-    for copy in sum_copies:
-        copy.wait_recv()
+    for peer in peers:
+        send, recv = energy_send.at[peer], energy_recv.at[peer]
+        remote(energy_own, energies.at[peer], send, recv, (g, peer)).wait_recv()
+    gathered = jnp.concatenate([energies[k] for k in range(freqs)], axis=0)
+    energy_ref[...] = gathered.T[:KMAX]
+
+    old = lax.broadcasted_iota(jnp.int32, (lanes, lanes), 0)
+    new = lax.broadcasted_iota(jnp.int32, (lanes, lanes), 1)
+    both = 2 * KMAX
+    moves = jnp.logical_and(old // both == lax.rem(new, freqs), lax.rem(old, both) == new // freqs)
+    moves = jnp.where(moves, 1.0, 0.0).astype(jnp.bfloat16)
+    for peer in peers:
+        send, recv = sum_send.at[peer], sum_recv.at[peer]
+        remote(sums.at[s], sums.at[peer], send, recv, (g, peer)).wait_recv()
     whole = sums[0]
     for place in range(1, n_space):
         whole = whole + sums[place]
-    coherence_ref[...] = whole / total
+    whole = whole / total
+    high = whole.astype(jnp.bfloat16).astype(jnp.float32)
+    mid = (whole - high).astype(jnp.bfloat16).astype(jnp.float32)
+    pieces = jnp.concatenate([high, mid, whole - high - mid, jnp.zeros_like(whole)], axis=0)
+    moved = jnp.dot(pieces.astype(jnp.bfloat16), moves, preferred_element_type=jnp.float32)
+    moved = moved[:KMAX] + (moved[KMAX : 2 * KMAX] + moved[2 * KMAX : 3 * KMAX])
+    for place in range(both):
+        piece = moved[:, place * freqs : (place + 1) * freqs]
+        coherence_ref[place // KMAX, place % KMAX] = piece
 
     @pl.loop(0, n_chips)
     def _(step):
@@ -402,6 +434,26 @@
     sends = row_copies + coef_copies + energy_copies + part_copies + sum_copies
     for copy in [weight_copy] + sends:
         copy.wait_send()
+
+
+def hand_on(modes_in, energy_in, coherence_in, modes_out, energy_out, coherence_out, held, ins, outs):
+    freqs = held.shape[0]
+
+    def taken(freq):
+        return pltpu.make_async_copy(modes_in.at[freq], held.at[freq], ins.at[freq])
+
+    def given(freq):
+        return pltpu.make_async_copy(held.at[freq], modes_out.at[freq], outs.at[freq])
+
+    for freq in range(freqs):
+        taken(freq).start()
+    energy_out[...] = energy_in[...]
+    coherence_out[...] = coherence_in[...]
+    for freq in range(freqs):
+        taken(freq).wait()
+        given(freq).start()
+    for freq in range(freqs):
+        given(freq).wait()
 
 
 def on_device(n_freq, n_space, spectra, weight, partner, counts):
@@ -418,8 +470,8 @@
         functools.partial(kernel, n_freq, n_space, points * n_space),
         out_shape=(
             jax.ShapeDtypeStruct((freqs, rows, points), bf16),
-            jax.ShapeDtypeStruct((freqs, KMAX, 128), f32),
-            jax.ShapeDtypeStruct((KMAX, lanes), f32),
+            jax.ShapeDtypeStruct((KMAX, freqs), f32),
+            jax.ShapeDtypeStruct((2, KMAX, KMAX, freqs), f32),
         ),
         in_specs=[
             pl.BlockSpec(memory_space=pl.ANY),
@@ -428,24 +480,22 @@
             pl.BlockSpec(memory_space=smem),
         ],
         out_specs=(
-            pl.BlockSpec(memory_space=pl.ANY),
+            pl.BlockSpec(memory_space=pltpu.HBM),
             pl.BlockSpec(memory_space=vmem),
             pl.BlockSpec(memory_space=vmem),
         ),
         scratch_shapes=[
             vmem((freqs, points, wide), bf16),
-            vmem((points, 128), f32),
-            vmem((points, wide), bf16),
             vmem((2 * n_chips, half, half), f32),
             vmem((n_chips, half, half), f32),
             vmem((n_chips, half, half), f32),
             vmem((rows, wide), bf16),
             vmem((freqs, rows, wide), bf16),
-            vmem((KMAX, 128), f32),
-            vmem((freqs, KMAX, 128), f32),
+            vmem((1, 128), f32),
+            vmem((freqs, 1, 128), f32),
             vmem((freqs, rows, points), bf16),
             vmem((4, freqs, rows, quarter), bf16),
-            vmem((4, 1, quarter), f32),
+            vmem((1, points), f32),
             vmem((1, quarter), f32),
             vmem((1, lanes), f32),
             vmem((4, 1, lanes), f32),
@@ -476,8 +526,23 @@
             collective_id=0, has_side_effects=True, vmem_limit_bytes=60 * 1024 * 1024
         ),
     )(spectra, weight.reshape(points // 128, 128), partner, counts)
-    coherence = coherence.reshape(KMAX, freqs, 2, KMAX).transpose(1, 2, 3, 0)
-    return modes, energy[:, :, 0], coherence
+    outs = (modes, energy, coherence)
+    modes, energy, coherence = pl.pallas_call(
+        hand_on,
+        out_shape=tuple(jax.ShapeDtypeStruct(out.shape, out.dtype) for out in outs),
+        in_specs=[
+            pl.BlockSpec(memory_space=pltpu.HBM),
+            pl.BlockSpec(memory_space=vmem),
+            pl.BlockSpec(memory_space=vmem),
+        ],
+        out_specs=(
+            pl.BlockSpec(memory_space=pltpu.HBM),
+            pl.BlockSpec(memory_space=vmem),
+            pl.BlockSpec(memory_space=vmem),
+        ),
+        scratch_shapes=[vmem(modes.shape, bf16), dma((freqs,)), dma((freqs,))],
+    )(*outs)
+    return modes, energy.T, coherence.transpose(3, 0, 1, 2)
 
 
 def solution(mesh):

time: 73.8 us -> 65.7 us (0.89)
  local copies, waits for them, and re-layouts: 5.9 us -> 0 us
  Pallas kernels: 67 us -> 64.8 us
    pallas_call x1, Pallas kernels: 67 us -> 61 us  [on_device(): pl.pallas_call(functools.partial(kernel, n_freq, n_space, points * n_spac...]
    pallas_call x0 -> x1, Pallas kernels: none -> 3.87 us  [on_device(): pl.pallas_call(hand_on, out_shape=tuple((jax.ShapeDtypeStruct(out.shape,...]
    unnamed x2 -> x0, local copies, waits for them, and re-layouts: 3.43 us -> none
    slice x1 -> x0, local copies, waits for them, and re-layouts: 1.55 us -> none  [on_device(): return (modes, energy[:, :, 0], coherence)]
    reshape x1 -> x0, local copies, waits for them, and re-layouts: 0.92 us -> none  [on_device(): coherence = coherence.reshape(KMAX, freqs, 2, KMAX).transpose(1, 2, 3, 0)]
where the time goes in v2:
time: 65.7 us; the launch traced here: 65.5 us
  Pallas kernels  64.8 us (99%)
    pallas_call x1, Pallas kernels, on_device(): pl.pallas_call(functools.partial(kernel, n_freq, n_space, points * n_spac...  61 us
    pallas_call x1, Pallas kernels, on_device(): pl.pallas_call(hand_on, out_shape=tuple((jax.ShapeDtypeStruct(out.shape,...  3.87 us

profile of v2, /device:TPU:1, one launch (start us, length us, event | category | flops | bytes accessed | tf_op | source)
XLA Modules:
  0.0 65.5 jit_solution(8651948486216655012)
XLA Ops:
  0.6 61.0 %shard_map.67 = (bf16[16,16,3072]{2,1,0:T(8,128)(2,1)}, f32[8,16]{1,0:T(8,128)}, f32[2,8,8,16]{3,2,1,0:T(8,128)}) custom-call(bf16[16,3072,256]{2,1,0:T(8,128)(2,1)} %spectra_hbm.1, f32[24,128]{1,0:T(8,128)} %bitcast.3, s32[16]{0:T(128)} %partner_ref.1, s32[16]{0:T(128)} %counts_ref.1), custom_call_target="tpu_custom_call" | custom-call | tf_op jit(solution)/shard_map/pallas_call | solution.py:469
  61.6 3.9 %shard_map.68 = (bf16[16,16,3072]{2,1,0:T(8,128)(2,1)}, f32[8,16]{1,0:T(8,128)}, f32[2,8,8,16]{3,2,1,0:T(8,128)}) custom-call(bf16[16,16,3072]{2,1,0:T(8,128)(2,1)} %get-tuple-element.9.modes_in, f32[8,16]{1,0:T(8,128)} %get-tuple-element.10.energy_in, f32[2,8,8,16]{3,2,1,0:T(8,128)} %get-tuple-element.11.coherence_in), custom_call_target="tpu_custom_call" | custom-call | tf_op jit(solution)/shard_map/pallas_call | solution.py:530

commit v3 on v2

--- a/solution.py
+++ b/solution.py
@@ -180,20 +180,25 @@
         to_y = lax.rem(y + lax.rem(ahead, n_y), n_y)
         return to_z * n_y + to_y
 
-    def chip_at(step):
-        return chip_ahead(n_chips - 1 - step)
+    def chip_at(k):
+        return chip_ahead(n_chips - 1 - k)
+
+    def place_at(step):
+        step = jnp.int32(step)
+        last = step == 2 * n_chips - 1
+        early = step < n_chips - 1
+        own_even = jnp.logical_or(early, last)
+        k_even = jnp.where(early, step, jnp.where(last, n_chips - 1, step - (n_chips - 1)))
+        own = jnp.where(core == 0, own_even.astype(jnp.int32), (step >= n_chips).astype(jnp.int32))
+        return own, jnp.where(core == 0, k_even, lax.rem(step, n_chips))
 
     def slot_at(step):
-        pair, second = step // 2, lax.rem(step, 2) == 1
-        early = jnp.where(pair == 0, 0, n_chips + pair - 1)
-        late = jnp.where(pair == n_chips - 1, 2 * n_chips - 1, pair + 1)
-        return jnp.where(second, late, early)
+        own, k = place_at(step)
+        return own * n_chips + k
 
     def freq_at(step):
-        slot = slot_at(step)
-        first = slot < n_chips
-        place = jnp.where(first, slot, slot - n_chips)
-        return 2 * chip_at(place) + jnp.where(first, 1 - core, core)
+        own, k = place_at(step)
+        return 2 * chip_at(k) + jnp.where(own == 1, core, 1 - core)
 
     def load(step):
         freq = freq_at(step)
@@ -246,24 +251,39 @@
         for step in steps:
             squares[slot_at(step)] = packed(moment(spectra[freq_at(step)], weight_row[...]))
 
-    def add_and_send(k):
-        core_copy(k).wait_recv()
-        squares[n_chips + k] = squares[n_chips + k] + from_core[k]
-        chip_copy(k).start()
+    def hand_over(step):
+        own, k = place_at(step)
+
+        @pl.when(own == 0)
+        def _():
+            core_copy(k).start()
+
+    def add_and_send(step):
+        own, k = place_at(step)
+
+        @pl.when(own == 1)
+        def _():
+            core_copy(k).wait_recv()
+            squares[n_chips + k] = squares[n_chips + k] + from_core[k]
+            chip_copy(k).start()
 
     gram(0, 1)
     pl.semaphore_wait(barrier, n_space - 1 + 3)
-    core_copy(0).start()
-    core_copy(1).start()
+    hand_over(0)
+    hand_over(1)
 
     @pl.loop(1, n_chips - 1)
     def _(pair):
         gram(2 * pair, 2 * pair + 1)
-        core_copy(pair + 1).start()
-        add_and_send(pair - 1)
+        hand_over(2 * pair)
+        hand_over(2 * pair + 1)
+        add_and_send(2 * pair - 2 + core)
+        add_and_send(2 * pair - 1 + core)
 
     gram(2 * n_chips - 2)
-    add_and_send(n_chips - 2)
+    hand_over(2 * n_chips - 2)
+    add_and_send(2 * n_chips - 4 + core)
+    add_and_send(2 * n_chips - 3 + core)
 
     start = pl.multiple_of(meeting(0)[1] * quarter, 128)
     weight_copy = remote(
@@ -334,10 +354,13 @@
 
     @pl.loop(0, freqs)
     def _(step):
+        even = step < n_chips + core
+        place = jnp.where(step == 0, 0, jnp.where(even, step - core, step - n_chips))
+        parity = jnp.where(step == 0, core, jnp.where(even, 0, 1))
         ahead = jnp.int32(near[0])
-        for place in range(1, n_chips):
-            ahead = jnp.where(step // 2 == place, near[place], ahead)
-        freq = 2 * chip_ahead(ahead) + lax.rem(core + step, 2)
+        for spot in range(1, n_chips):
+            ahead = jnp.where(place == spot, near[spot], ahead)
+        freq = 2 * chip_ahead(ahead) + parity
 
         @pl.when(step > 0)
         def _():
@@ -436,24 +459,25 @@
         copy.wait_send()
 
 
-def hand_on(modes_in, energy_in, coherence_in, modes_out, energy_out, coherence_out, held, ins, outs):
-    freqs = held.shape[0]
-
-    def taken(freq):
-        return pltpu.make_async_copy(modes_in.at[freq], held.at[freq], ins.at[freq])
-
-    def given(freq):
-        return pltpu.make_async_copy(held.at[freq], modes_out.at[freq], outs.at[freq])
-
-    for freq in range(freqs):
-        taken(freq).start()
-    energy_out[...] = energy_in[...]
-    coherence_out[...] = coherence_in[...]
-    for freq in range(freqs):
-        taken(freq).wait()
-        given(freq).start()
-    for freq in range(freqs):
-        given(freq).wait()
+def hand_on(*refs):
+    sources, targets, held = refs[:3], refs[3:6], refs[6:9]
+    small, modes = (1, 2), range(held[0].shape[0])
+    ins, outs = refs[9:]
+
+    def copies(start, end, sems):
+        rows = [pltpu.make_async_copy(start[k], end[k], sems.at[k]) for k in small]
+        for freq in modes:
+            rows.append(pltpu.make_async_copy(start[0].at[freq], end[0].at[freq], sems.at[3 + freq]))
+        return rows
+
+    taken, given = copies(sources, held, ins), copies(held, targets, outs)
+    for copy in taken:
+        copy.start()
+    for first, second in zip(taken, given):
+        first.wait()
+        second.start()
+    for copy in given:
+        copy.wait()
 
 
 def on_device(n_freq, n_space, spectra, weight, partner, counts):
@@ -530,17 +554,10 @@
     modes, energy, coherence = pl.pallas_call(
         hand_on,
         out_shape=tuple(jax.ShapeDtypeStruct(out.shape, out.dtype) for out in outs),
-        in_specs=[
-            pl.BlockSpec(memory_space=pltpu.HBM),
-            pl.BlockSpec(memory_space=vmem),
-            pl.BlockSpec(memory_space=vmem),
-        ],
-        out_specs=(
-            pl.BlockSpec(memory_space=pltpu.HBM),
-            pl.BlockSpec(memory_space=vmem),
-            pl.BlockSpec(memory_space=vmem),
-        ),
-        scratch_shapes=[vmem(modes.shape, bf16), dma((freqs,)), dma((freqs,))],
+        in_specs=[pl.BlockSpec(memory_space=pltpu.HBM)] * 3,
+        out_specs=(pl.BlockSpec(memory_space=pltpu.HBM),) * 3,
+        scratch_shapes=[vmem(out.shape, out.dtype) for out in outs]
+        + [dma((3 + freqs,)), dma((3 + freqs,))],
     )(*outs)
     return modes, energy.T, coherence.transpose(3, 0, 1, 2)
 

time: 65.7 us -> 62.2 us (0.947)
  Pallas kernels: 64.8 us -> 61.4 us
    pallas_call x1, Pallas kernels: 61 us -> 58.9 us  [on_device(): pl.pallas_call(functools.partial(kernel, n_freq, n_space, points * n_spac...]
    pallas_call x1, Pallas kernels: 3.87 us -> 2.47 us  [on_device(): pl.pallas_call(hand_on, out_shape=tuple((jax.ShapeDtypeStruct(out.shape,...]
where the time goes in v3:
time: 62.2 us; the launch traced here: 62 us
  Pallas kernels  61.4 us (99%)
  between operations  0.64 us (1%)
    pallas_call x1, Pallas kernels, on_device(): pl.pallas_call(functools.partial(kernel, n_freq, n_space, points * n_spac...  58.9 us
    pallas_call x1, Pallas kernels, on_device(): pl.pallas_call(hand_on, out_shape=tuple((jax.ShapeDtypeStruct(out.shape,...  2.47 us

profile of v3, /device:TPU:1, one launch (start us, length us, event | category | flops | bytes accessed | tf_op | source)
XLA Modules:
  0.0 62.0 jit_solution(14066237177394420498)
XLA Ops:
  0.6 58.9 %shard_map.67 = (bf16[16,16,3072]{2,1,0:T(8,128)(2,1)}, f32[8,16]{1,0:T(8,128)}, f32[2,8,8,16]{3,2,1,0:T(8,128)}) custom-call(bf16[16,3072,256]{2,1,0:T(8,128)(2,1)} %spectra_hbm.1, f32[24,128]{1,0:T(8,128)} %bitcast.3, s32[16]{0:T(128)} %partner_ref.1, s32[16]{0:T(128)} %counts_ref.1), custom_call_target="tpu_custom_call" | custom-call | tf_op jit(solution)/shard_map/pallas_call | solution.py:493
  59.5 2.5 %shard_map.68 = (bf16[16,16,3072]{2,1,0:T(8,128)(2,1)}, f32[8,16]{1,0:T(8,128)}, f32[2,8,8,16]{3,2,1,0:T(8,128)}) custom-call(bf16[16,16,3072]{2,1,0:T(8,128)(2,1)} %get-tuple-element.9.refs_0_, f32[8,16]{1,0:T(8,128)} %get-tuple-element.10.refs_1_, f32[2,8,8,16]{3,2,1,0:T(8,128)} %get-tuple-element.11.refs_2_), custom_call_target="tpu_custom_call" | custom-call | tf_op jit(solution)/shard_map/pallas_call | solution.py:554

commit v4 on v3

--- a/solution.py
+++ b/solution.py
@@ -11,6 +11,7 @@
 ITERS = 4
 EPS = 1e-06
 AHEAD = 5
+EARLY = 1
 MESH = pl.DeviceIdType.MESH
 HIGHEST = lax.Precision.HIGHEST
 
@@ -86,14 +87,14 @@
     ranks = lax.broadcasted_iota(jnp.int32, (KMAX, 1), 0)
     scale = jnp.where(ranks < count, lax.rsqrt(energy + EPS), 0.0)
     part_re, part_im = vec_re * scale, vec_im * scale
-    coefficient = jnp.concatenate(
-        [
-            jnp.concatenate([part_re, -part_im], axis=1),
-            jnp.concatenate([part_im, part_re], axis=1),
-        ],
-        axis=0,
-    )
-    return coefficient.astype(jnp.bfloat16), energy
+    return jnp.concatenate([part_re, -part_im], axis=1).astype(jnp.bfloat16), energy
+
+
+def both_halves(upper):
+    half = upper.shape[1] // 2
+    upper = upper.astype(jnp.float32)
+    lower = jnp.concatenate([-upper[:, half:], upper[:, :half]], axis=1)
+    return jnp.concatenate([upper, lower], axis=0).astype(jnp.bfloat16)
 
 
 def kernel(
@@ -148,6 +149,7 @@
     quarter = points // 4
     g, s = lax.axis_index("freq"), lax.axis_index("space")
     core, chip = lax.rem(s, 2), s // 2
+    late = core if EARLY == 0 else 1 - core
     n_chips = n_space // 2
     n_y = max(n_chips // 2, 1)
     z_lo, y = chip // n_y, lax.rem(chip, n_y)
@@ -187,10 +189,11 @@
         step = jnp.int32(step)
         last = step == 2 * n_chips - 1
         early = step < n_chips - 1
-        own_even = jnp.logical_or(early, last)
-        k_even = jnp.where(early, step, jnp.where(last, n_chips - 1, step - (n_chips - 1)))
-        own = jnp.where(core == 0, own_even.astype(jnp.int32), (step >= n_chips).astype(jnp.int32))
-        return own, jnp.where(core == 0, k_even, lax.rem(step, n_chips))
+        own_first = jnp.logical_or(early, last)
+        k_first = jnp.where(early, step, jnp.where(last, n_chips - 1, step - (n_chips - 1)))
+        own_last = step >= n_chips
+        own = jnp.where(late == 0, own_first.astype(jnp.int32), own_last.astype(jnp.int32))
+        return own, jnp.where(late == 0, k_first, lax.rem(step, n_chips))
 
     def slot_at(step):
         own, k = place_at(step)
@@ -277,13 +280,13 @@
         gram(2 * pair, 2 * pair + 1)
         hand_over(2 * pair)
         hand_over(2 * pair + 1)
-        add_and_send(2 * pair - 2 + core)
-        add_and_send(2 * pair - 1 + core)
+        add_and_send(2 * pair - 2 + late)
+        add_and_send(2 * pair - 1 + late)
 
     gram(2 * n_chips - 2)
     hand_over(2 * n_chips - 2)
-    add_and_send(2 * n_chips - 4 + core)
-    add_and_send(2 * n_chips - 3 + core)
+    add_and_send(2 * n_chips - 4 + late)
+    add_and_send(2 * n_chips - 3 + late)
 
     start = pl.multiple_of(meeting(0)[1] * quarter, 128)
     weight_copy = remote(
@@ -319,8 +322,18 @@
     energies[s] = energy
 
     near = [ahead for ahead in (0, 1, 3, 4, 2, 5, 7, 6) if ahead < n_chips]
-    peers = [2 * chip_ahead(ahead) + lax.rem(core + flip, 2) for ahead in near for flip in (0, 1)]
-    peers = peers[1:]
+
+    def near_freq(place, parity):
+        ahead = jnp.int32(near[0])
+        for spot in range(1, n_chips):
+            ahead = jnp.where(place == spot, near[spot], ahead)
+        return 2 * chip_ahead(ahead) + parity
+
+    peers = []
+    for item in range(n_space - 1):
+        first = item < n_chips - 1 + late
+        place = jnp.where(first, item + 1 - late, item - (n_chips - 1))
+        peers.append(near_freq(place, jnp.where(first, EARLY, 1 - EARLY)))
 
     def coef_copy(peer, owner):
         send, recv = coef_send.at[peer], coef_recv.at[owner]
@@ -354,19 +367,16 @@
 
     @pl.loop(0, freqs)
     def _(step):
-        even = step < n_chips + core
-        place = jnp.where(step == 0, 0, jnp.where(even, step - core, step - n_chips))
-        parity = jnp.where(step == 0, core, jnp.where(even, 0, 1))
-        ahead = jnp.int32(near[0])
-        for spot in range(1, n_chips):
-            ahead = jnp.where(place == spot, near[spot], ahead)
-        freq = 2 * chip_ahead(ahead) + parity
+        first = step < n_chips + late
+        place = jnp.where(step == 0, 0, jnp.where(first, step - late, step - n_chips))
+        parity = jnp.where(step == 0, core, jnp.where(first, EARLY, 1 - EARLY))
+        freq = near_freq(place, parity)
 
         @pl.when(step > 0)
         def _():
             coef_copy(freq, freq).wait_recv()
 
-        modes[freq] = times_transposed(coefs[freq], spectra[freq]).astype(jnp.bfloat16)
+        modes[freq] = times_transposed(both_halves(coefs[freq]), spectra[freq]).astype(jnp.bfloat16)
         for slot in (2, 3, 0, 1):
             mode_copy(freq, slot).start()
         mode_store(freq).start()
@@ -386,7 +396,7 @@
     is_re = lax.rem(lax.broadcasted_iota(jnp.int32, (KMAX, rows), 1), 2 * KMAX) < KMAX
     line = weight_in[...]
     part_copies = []
-    for slot in range(4):
+    for slot in (2, 3, 0, 1):
         phi = arrived[slot].reshape(rows, quarter)
         psi = arrived[3 - slot].reshape(rows, quarter)
         wpsi = (psi.astype(jnp.float32) * line).astype(jnp.bfloat16)
@@ -419,26 +429,13 @@
     gathered = jnp.concatenate([energies[k] for k in range(freqs)], axis=0)
     energy_ref[...] = gathered.T[:KMAX]
 
-    old = lax.broadcasted_iota(jnp.int32, (lanes, lanes), 0)
-    new = lax.broadcasted_iota(jnp.int32, (lanes, lanes), 1)
-    both = 2 * KMAX
-    moves = jnp.logical_and(old // both == lax.rem(new, freqs), lax.rem(old, both) == new // freqs)
-    moves = jnp.where(moves, 1.0, 0.0).astype(jnp.bfloat16)
     for peer in peers:
         send, recv = sum_send.at[peer], sum_recv.at[peer]
         remote(sums.at[s], sums.at[peer], send, recv, (g, peer)).wait_recv()
     whole = sums[0]
     for place in range(1, n_space):
         whole = whole + sums[place]
-    whole = whole / total
-    high = whole.astype(jnp.bfloat16).astype(jnp.float32)
-    mid = (whole - high).astype(jnp.bfloat16).astype(jnp.float32)
-    pieces = jnp.concatenate([high, mid, whole - high - mid, jnp.zeros_like(whole)], axis=0)
-    moved = jnp.dot(pieces.astype(jnp.bfloat16), moves, preferred_element_type=jnp.float32)
-    moved = moved[:KMAX] + (moved[KMAX : 2 * KMAX] + moved[2 * KMAX : 3 * KMAX])
-    for place in range(both):
-        piece = moved[:, place * freqs : (place + 1) * freqs]
-        coherence_ref[place // KMAX, place % KMAX] = piece
+    coherence_ref[...] = whole / total
 
     @pl.loop(0, n_chips)
     def _(step):
@@ -459,24 +456,55 @@
         copy.wait_send()
 
 
-def hand_on(*refs):
-    sources, targets, held = refs[:3], refs[3:6], refs[6:9]
-    small, modes = (1, 2), range(held[0].shape[0])
-    ins, outs = refs[9:]
-
-    def copies(start, end, sems):
-        rows = [pltpu.make_async_copy(start[k], end[k], sems.at[k]) for k in small]
-        for freq in modes:
-            rows.append(pltpu.make_async_copy(start[0].at[freq], end[0].at[freq], sems.at[3 + freq]))
-        return rows
-
-    taken, given = copies(sources, held, ins), copies(held, targets, outs)
-    for copy in taken:
+def with_freq_last(value, freqs):
+    lanes, both = value.shape[1], 2 * KMAX
+    old = lax.broadcasted_iota(jnp.int32, (lanes, lanes), 0)
+    new = lax.broadcasted_iota(jnp.int32, (lanes, lanes), 1)
+    moves = jnp.logical_and(old // both == lax.rem(new, freqs), lax.rem(old, both) == new // freqs)
+    moves = jnp.where(moves, 1.0, 0.0).astype(jnp.bfloat16)
+    high = value.astype(jnp.bfloat16).astype(jnp.float32)
+    mid = (value - high).astype(jnp.bfloat16).astype(jnp.float32)
+    pieces = jnp.concatenate([high, mid, value - high - mid, jnp.zeros_like(value)], axis=0)
+    moved = jnp.dot(pieces.astype(jnp.bfloat16), moves, preferred_element_type=jnp.float32)
+    return moved[:KMAX] + (moved[KMAX:both] + moved[both : both + KMAX])
+
+
+def hand_on(modes_in, energy_in, coherence_in, modes_out, energy_out, coherence_out, *scratch):
+    modes, energy, coherence, spread, ins, outs = scratch
+    freqs = modes.shape[0]
+
+    def taken(freq):
+        return pltpu.make_async_copy(modes_in.at[freq], modes.at[freq], ins.at[freq])
+
+    def given(freq):
+        return pltpu.make_async_copy(modes.at[freq], modes_out.at[freq], outs.at[freq])
+
+    small_in = [
+        pltpu.make_async_copy(coherence_in, coherence, ins.at[freqs]),
+        pltpu.make_async_copy(energy_in, energy, ins.at[freqs + 1]),
+    ]
+    small_out = [
+        pltpu.make_async_copy(spread, coherence_out, outs.at[freqs]),
+        pltpu.make_async_copy(energy, energy_out, outs.at[freqs + 1]),
+    ]
+    for copy in small_in:
         copy.start()
-    for first, second in zip(taken, given):
-        first.wait()
-        second.start()
-    for copy in given:
+    for freq in range(freqs):
+        taken(freq).start()
+    for copy in small_in:
+        copy.wait()
+    small_out[1].start()
+    moved = with_freq_last(coherence[...], freqs)
+    for place in range(2 * KMAX):
+        piece = moved[:, place * freqs : (place + 1) * freqs]
+        spread[place // KMAX, place % KMAX] = piece
+    for freq in range(freqs):
+        taken(freq).wait()
+        given(freq).start()
+    small_out[0].start()
+    for freq in range(freqs):
+        given(freq).wait()
+    for copy in small_out:
         copy.wait()
 
 
@@ -495,7 +523,7 @@
         out_shape=(
             jax.ShapeDtypeStruct((freqs, rows, points), bf16),
             jax.ShapeDtypeStruct((KMAX, freqs), f32),
-            jax.ShapeDtypeStruct((2, KMAX, KMAX, freqs), f32),
+            jax.ShapeDtypeStruct((KMAX, lanes), f32),
         ),
         in_specs=[
             pl.BlockSpec(memory_space=pl.ANY),
@@ -513,8 +541,8 @@
             vmem((2 * n_chips, half, half), f32),
             vmem((n_chips, half, half), f32),
             vmem((n_chips, half, half), f32),
-            vmem((rows, wide), bf16),
-            vmem((freqs, rows, wide), bf16),
+            vmem((KMAX, wide), bf16),
+            vmem((freqs, KMAX, wide), bf16),
             vmem((1, 128), f32),
             vmem((freqs, 1, 128), f32),
             vmem((freqs, rows, points), bf16),
@@ -550,15 +578,25 @@
             collective_id=0, has_side_effects=True, vmem_limit_bytes=60 * 1024 * 1024
         ),
     )(spectra, weight.reshape(points // 128, 128), partner, counts)
-    outs = (modes, energy, coherence)
+    last = jax.ShapeDtypeStruct((2, KMAX, KMAX, freqs), f32)
     modes, energy, coherence = pl.pallas_call(
         hand_on,
-        out_shape=tuple(jax.ShapeDtypeStruct(out.shape, out.dtype) for out in outs),
+        out_shape=(
+            jax.ShapeDtypeStruct(modes.shape, bf16),
+            jax.ShapeDtypeStruct(energy.shape, f32),
+            last,
+        ),
         in_specs=[pl.BlockSpec(memory_space=pltpu.HBM)] * 3,
         out_specs=(pl.BlockSpec(memory_space=pltpu.HBM),) * 3,
-        scratch_shapes=[vmem(out.shape, out.dtype) for out in outs]
-        + [dma((3 + freqs,)), dma((3 + freqs,))],
-    )(*outs)
+        scratch_shapes=[
+            vmem(modes.shape, bf16),
+            vmem(energy.shape, f32),
+            vmem(coherence.shape, f32),
+            vmem(last.shape, f32),
+            dma((freqs + 2,)),
+            dma((freqs + 2,)),
+        ],
+    )(modes, energy, coherence)
     return modes, energy.T, coherence.transpose(3, 0, 1, 2)
 
 

time: 62.2 us -> 61 us (0.981)
  Pallas kernels: 61.4 us -> 60.1 us
    pallas_call x1, Pallas kernels: 58.9 us -> 57.7 us  [on_device(): pl.pallas_call(functools.partial(kernel, n_freq, n_space, points * n_spac...]
where the time goes in v4:
time: 61 us; the launch traced here: 60.8 us
  Pallas kernels  60.1 us (99%)
  between operations  0.64 us (1%)
    pallas_call x1, Pallas kernels, on_device(): pl.pallas_call(functools.partial(kernel, n_freq, n_space, points * n_spac...  57.7 us
    pallas_call x1, Pallas kernels, on_device(): pl.pallas_call(hand_on, out_shape=(jax.ShapeDtypeStruct(modes.shape, bf16...  2.47 us

profile of v4, /device:TPU:1, one launch (start us, length us, event | category | flops | bytes accessed | tf_op | source)
XLA Modules:
  0.0 60.8 jit_solution(17605986589465820850)
XLA Ops:
  0.6 57.7 %shard_map.67 = (bf16[16,16,3072]{2,1,0:T(8,128)(2,1)}, f32[8,16]{1,0:T(8,128)}, f32[8,256]{1,0:T(8,128)}) custom-call(bf16[16,3072,256]{2,1,0:T(8,128)(2,1)} %spectra_hbm.1, f32[24,128]{1,0:T(8,128)} %bitcast.3, s32[16]{0:T(128)} %partner_ref.1, s32[16]{0:T(128)} %counts_ref.1), custom_call_target="tpu_custom_call" | custom-call | tf_op jit(solution)/shard_map/pallas_call | solution.py:521
  58.3 2.5 %shard_map.68 = (bf16[16,16,3072]{2,1,0:T(8,128)(2,1)}, f32[8,16]{1,0:T(8,128)}, f32[2,8,8,16]{3,2,1,0:T(8,128)}) custom-call(bf16[16,16,3072]{2,1,0:T(8,128)(2,1)} %get-tuple-element.9.modes_in, f32[8,16]{1,0:T(8,128)} %get-tuple-element.10.energy_in, f32[8,256]{1,0:T(8,128)} %get-tuple-element.11.coherence_in), custom_call_target="tpu_custom_call" | custom-call | tf_op jit(solution)/shard_map/pallas_call | solution.py:582

commit v5 on v4

--- a/solution.py
+++ b/solution.py
@@ -283,7 +283,7 @@
         add_and_send(2 * pair - 2 + late)
         add_and_send(2 * pair - 1 + late)
 
-    gram(2 * n_chips - 2)
+    gram(2 * n_chips - 2, 2 * n_chips - 1)
     hand_over(2 * n_chips - 2)
     add_and_send(2 * n_chips - 4 + late)
     add_and_send(2 * n_chips - 3 + late)
@@ -306,7 +306,6 @@
     for copy in row_copies:
         copy.start()
 
-    gram(2 * n_chips - 1)
     core_copy(n_chips - 1).wait_recv()
     square = squares[2 * n_chips - 1] + from_core[n_chips - 1]
     for step in range(n_chips - 1):
@@ -472,12 +471,15 @@
 def hand_on(modes_in, energy_in, coherence_in, modes_out, energy_out, coherence_out, *scratch):
     modes, energy, coherence, spread, ins, outs = scratch
     freqs = modes.shape[0]
-
-    def taken(freq):
-        return pltpu.make_async_copy(modes_in.at[freq], modes.at[freq], ins.at[freq])
-
-    def given(freq):
-        return pltpu.make_async_copy(modes.at[freq], modes_out.at[freq], outs.at[freq])
+    many = freqs // 4
+
+    def taken(part):
+        rows = pl.ds(part * many, many)
+        return pltpu.make_async_copy(modes_in.at[rows], modes.at[rows], ins.at[part])
+
+    def given(part):
+        rows = pl.ds(part * many, many)
+        return pltpu.make_async_copy(modes.at[rows], modes_out.at[rows], outs.at[part])
 
     small_in = [
         pltpu.make_async_copy(coherence_in, coherence, ins.at[freqs]),
@@ -489,8 +491,8 @@
     ]
     for copy in small_in:
         copy.start()
-    for freq in range(freqs):
-        taken(freq).start()
+    for part in range(4):
+        taken(part).start()
     for copy in small_in:
         copy.wait()
     small_out[1].start()
@@ -498,12 +500,12 @@
     for place in range(2 * KMAX):
         piece = moved[:, place * freqs : (place + 1) * freqs]
         spread[place // KMAX, place % KMAX] = piece
-    for freq in range(freqs):
-        taken(freq).wait()
-        given(freq).start()
+    for part in range(4):
+        taken(part).wait()
+        given(part).start()
     small_out[0].start()
-    for freq in range(freqs):
-        given(freq).wait()
+    for part in range(4):
+        given(part).wait()
     for copy in small_out:
         copy.wait()
 

time: 61 us -> 60.3 us (0.989)
  Pallas kernels: 60.1 us -> 59.4 us
    pallas_call x1, Pallas kernels: 57.7 us -> 57 us  [on_device(): pl.pallas_call(functools.partial(kernel, n_freq, n_space, points * n_spac...]
where the time goes in v5:
time: 60.3 us; the launch traced here: 60.1 us
  Pallas kernels  59.4 us (99%)
  between operations  0.64 us (1%)
    pallas_call x1, Pallas kernels, on_device(): pl.pallas_call(functools.partial(kernel, n_freq, n_space, points * n_spac...  57 us
    pallas_call x1, Pallas kernels, on_device(): pl.pallas_call(hand_on, out_shape=(jax.ShapeDtypeStruct(modes.shape, bf16...  2.48 us

profile of v5, /device:TPU:1, one launch (start us, length us, event | category | flops | bytes accessed | tf_op | source)
XLA Modules:
  0.0 60.1 jit_solution(16579614160818896033)
XLA Ops:
  0.6 57.0 %shard_map.67 = (bf16[16,16,3072]{2,1,0:T(8,128)(2,1)}, f32[8,16]{1,0:T(8,128)}, f32[8,256]{1,0:T(8,128)}) custom-call(bf16[16,3072,256]{2,1,0:T(8,128)(2,1)} %spectra_hbm.1, f32[24,128]{1,0:T(8,128)} %bitcast.3, s32[16]{0:T(128)} %partner_ref.1, s32[16]{0:T(128)} %counts_ref.1), custom_call_target="tpu_custom_call" | custom-call | tf_op jit(solution)/shard_map/pallas_call | solution.py:523
  57.6 2.5 %shard_map.68 = (bf16[16,16,3072]{2,1,0:T(8,128)(2,1)}, f32[8,16]{1,0:T(8,128)}, f32[2,8,8,16]{3,2,1,0:T(8,128)}) custom-call(bf16[16,16,3072]{2,1,0:T(8,128)(2,1)} %get-tuple-element.9.modes_in, f32[8,16]{1,0:T(8,128)} %get-tuple-element.10.energy_in, f32[8,256]{1,0:T(8,128)} %get-tuple-element.11.coherence_in), custom_call_target="tpu_custom_call" | custom-call | tf_op jit(solution)/shard_map/pallas_call | solution.py:584
